TPU v7x, 32 devices: a whole 2x2x4 slice. The times are simulated.
32 devices in a mesh: gx: 4 (over x, core), gy: 8 (over z, y).
Axes of the slice: x: 2, y: 2, z: 4, core: 2. Of those that a mesh axis runs over, the one named last changes fastest.
Arguments:
- feats: bfloat16 [1024, 128, 128], P(('gx', 'gy')), may hold values from -24 to 24
- z_count: int32 [32], P(('gx', 'gy')), may hold values from 8 to 32
- hil_dest: int32 [1024], P(('gx', 'gy')), may hold values from 0 to 1023, as said below
- pool_group: int32 [1024, 128], P(('gx', 'gy')), may hold values from 0 to 31, never falling along the last dimension, each value on 1 to 8 neighbouring positions
- z_qkv: bfloat16 [128, 384], replicated, may hold values from -9.0156115 to 9.0156115
- z_proj: bfloat16 [128, 128], replicated, may hold values from -0.5 to 0.5
- z_up: bfloat16 [128, 512], replicated, may hold values from -0.5 to 0.5
- z_down: bfloat16 [512, 128], replicated, may hold values from -0.25 to 0.25
- z_gain: float32 [2, 128], replicated, may hold values from 0.1 to 1.9
- pool_w: bfloat16 [128, 256], replicated, may hold values from -0.5 to 0.5
- bn_gain: float32 [256], replicated, may hold values from 0.1 to 1.9
- p_qkv: bfloat16 [256, 768], replicated, may hold values from -6.375 to 6.375
- p_proj: bfloat16 [256, 256], replicated, may hold values from -0.375 to 0.375
- p_up: bfloat16 [256, 1024], replicated, may hold values from -0.375 to 0.375
- p_down: bfloat16 [1024, 256], replicated, may hold values from -0.1875 to 0.1875
- p_gain: float32 [2, 256], replicated, may hold values from 0.1 to 1.9
- unpool_w: bfloat16 [256, 128], replicated, may hold values from -0.375 to 0.375
Outputs:
- out: bfloat16 [1024, 128, 128], P(('gx', 'gy'))
Inputs may be any that keep to these rules, and one draw needn't show every extreme that they name: `hil_dest`: A permutation of 0 to 1023; value v stands for slot v % 32 of device v // 32, devices numbered gx index times the size of gy plus gy index. A cell stays on devices of its own gx index; of one device's 32 cells, each device of its gx index receives either none or exactly 8. `pool_group`: within each cell the numbers never fall, and each of 0 to 31 names 1 to 8 points.
All inputs are finite; a program needn't handle non-finite values.
Results may differ from a plain program's by a relative error of at most 0.018.
The roundings to bfloat16 on the way count: a program that leaves them out, or rounds other values in their place, can miss the bound.
Values may be sent and summed in bfloat16 or wider, within the bound.
A program may use at most 192 MiB of HBM per device.

v0:
```python
import math

import jax
import jax.numpy as jnp
from jax import lax
from jax.sharding import PartitionSpec as P

HEAD = 16
PGROUP = 32
PATCH = 1024


EPSILON = 1e-05
MASKED = -1e30


def normed(values, weight_gain):
    average = jnp.mean(values, axis=-1, keepdims=True)
    centred = values - average
    spread = jnp.mean(centred * centred, axis=-1, keepdims=True)
    return (centred * lax.rsqrt(spread + EPSILON) * weight_gain).astype(jnp.bfloat16)


def attend_patch(queries, keys_in, values, keep_mask):
    patch_rows = queries.shape[0]
    head_count = queries.shape[1]
    query_rows = min(512, patch_rows)
    head_group = 4
    score_scale = 1.0 / math.sqrt(queries.shape[2])
    row_blocks = []
    for row_start in range(0, patch_rows, query_rows):
        head_parts = []
        for head_start in range(0, head_count, head_group):
            scores = (
                jnp.einsum(
                    "qhd,khd->hqk",
                    queries[
                        row_start : row_start + query_rows, head_start : head_start + head_group
                    ],
                    keys_in[:, head_start : head_start + head_group],
                    preferred_element_type=jnp.float32,
                )
                * score_scale
            )
            scores = jnp.where(keep_mask[None, None, :], scores, MASKED)
            row_max = jnp.max(scores, axis=-1, keepdims=True)
            exponent = jnp.exp(scores - row_max)
            weights = (exponent / jnp.sum(exponent, axis=-1, keepdims=True)).astype(jnp.bfloat16)
            head_parts.append(
                jnp.einsum(
                    "hqk,khd->qhd",
                    weights,
                    values[:, head_start : head_start + head_group],
                    preferred_element_type=jnp.float32,
                ).astype(jnp.bfloat16)
            )
        row_blocks.append(jnp.concatenate(head_parts, axis=1))
    return jnp.concatenate(row_blocks, axis=0)


def one_patch(inputs):
    packed, keep_here = inputs
    return attend_patch(packed[:, 0], packed[:, 1], packed[:, 2], keep_here)


def run_block(rows_in, keep_mask, gain_rows, w_qkv, w_proj, w_up, w_down, patch_rows):
    row_count, feature_width = rows_in.shape
    head_count = feature_width // HEAD
    rows_float = rows_in.astype(jnp.float32)
    normal_one = normed(rows_float, gain_rows[0])
    projected = jnp.dot(normal_one, w_qkv, preferred_element_type=jnp.float32).astype(jnp.bfloat16)
    projected = projected.reshape(row_count // patch_rows, patch_rows, 3, head_count, HEAD)
    keep_rows = keep_mask.reshape(row_count // patch_rows, patch_rows)
    attended = lax.map(one_patch, (projected, keep_rows)).reshape(row_count, feature_width)
    middle = rows_float + jnp.dot(attended, w_proj, preferred_element_type=jnp.float32)
    normal_two = normed(middle, gain_rows[1])
    hidden = jax.nn.gelu(
        jnp.dot(normal_two, w_up, preferred_element_type=jnp.float32), approximate=False
    ).astype(jnp.bfloat16)
    return (middle + jnp.dot(hidden, w_down, preferred_element_type=jnp.float32)).astype(
        jnp.bfloat16
    )


def running_max(earlier, later):
    joined = jnp.where(earlier[1] == later[1], jnp.maximum(earlier[0], later[0]), later[0])
    return (joined, later[1])


def pick_rows(cell_rows, row_index):
    return cell_rows[row_index]


def shards(
    feats,
    z_count,
    hil_dest,
    pool_group,
    z_qkv,
    z_proj,
    z_up,
    z_down,
    z_gain,
    pool_w,
    bn_gain,
    p_qkv,
    p_proj,
    p_up,
    p_down,
    p_gain,
    unpool_w,
):
    cell_count, cell_points, feature_width = feats.shape
    pooled_width = pool_w.shape[1]
    row_devices = lax.axis_size("gy")
    capacity = 2 * cell_count // row_devices
    buffer_cells = row_devices * capacity
    cell_ids = jnp.arange(cell_count, dtype=jnp.int32)
    live_z = cell_ids < z_count[0]
    z_out = run_block(
        feats.reshape(cell_count * cell_points, feature_width),
        jnp.repeat(live_z, cell_points),
        z_gain,
        z_qkv,
        z_proj,
        z_up,
        z_down,
        PATCH,
    )
    z_out = z_out.reshape(cell_count, cell_points, feature_width)
    target_device = hil_dest // cell_count % row_devices
    target_slot = hil_dest % cell_count
    same_target = target_device[:, None] == target_device[None, :]
    earlier_cell = cell_ids[None, :] < cell_ids[:, None]
    target_rank = jnp.sum((same_target & earlier_cell).astype(jnp.int32), axis=1)
    position = target_device * capacity + target_rank
    matched = position[None, :] == jnp.arange(buffer_cells, dtype=jnp.int32)[:, None]
    occupied = jnp.any(matched, axis=1)
    source_cell = jnp.sum(jnp.where(matched, cell_ids[None, :], 0), axis=1)
    outgoing = jnp.where(
        occupied[:, None, None], jnp.take(z_out, source_cell, axis=0), jnp.zeros((), jnp.bfloat16)
    )
    outgoing_slot = jnp.where(occupied, target_slot[source_cell], -1)
    outgoing_live = jnp.where(occupied, live_z[source_cell].astype(jnp.int32), 0)
    incoming, incoming_slot, incoming_live = (
        lax.all_to_all(outgoing, "gy", split_axis=0, concat_axis=0, tiled=True),
        lax.all_to_all(outgoing_slot, "gy", split_axis=0, concat_axis=0, tiled=True),
        lax.all_to_all(outgoing_live, "gy", split_axis=0, concat_axis=0, tiled=True),
    )
    slot_match = incoming_slot[None, :] == cell_ids[:, None]
    anchor = jnp.sum(
        jnp.where(slot_match, jnp.arange(buffer_cells, dtype=jnp.int32)[None, :], 0), axis=1
    )
    h_cells = jnp.take(incoming, anchor, axis=0)
    live_h = jnp.take(incoming_live, anchor) > 0
    y_cells = jnp.dot(
        h_cells.reshape(cell_count * cell_points, feature_width),
        pool_w,
        preferred_element_type=jnp.float32,
    )
    y_cells = y_cells.reshape(cell_count, cell_points, pooled_width)
    scanned, _ = lax.associative_scan(running_max, (y_cells, pool_group[:, :, None]), axis=1)
    group_ends = (
        jnp.sum(
            (pool_group[:, None, :] <= jnp.arange(PGROUP, dtype=jnp.int32)[None, :, None]).astype(
                jnp.int32
            ),
            axis=2,
        )
        - 1
    )
    pooled_max = jax.vmap(pick_rows)(scanned, group_ends)
    live_weight = live_h.astype(jnp.float32)[:, None, None]
    local_count = jnp.sum(live_h.astype(jnp.float32)) * PGROUP
    local_sum = jnp.sum(live_weight * pooled_max, axis=(0, 1))
    local_square = jnp.sum(live_weight * pooled_max * pooled_max, axis=(0, 1))
    total_sum, total_square, live_count = lax.psum(
        (local_sum, local_square, local_count), ("gx", "gy")
    )
    average = total_sum / live_count
    variance = total_square / live_count - average * average
    pooled = jax.nn.gelu(
        (pooled_max - average) * lax.rsqrt(variance + EPSILON) * bn_gain, approximate=False
    ).astype(jnp.bfloat16)
    pooled = pooled.reshape(cell_count * PGROUP, pooled_width)
    p_out = run_block(
        pooled, jnp.repeat(live_h, PGROUP), p_gain, p_qkv, p_proj, p_up, p_down, PATCH
    )
    lifted = jnp.dot(p_out, unpool_w, preferred_element_type=jnp.float32).reshape(
        cell_count, PGROUP, feature_width
    )
    sent_back = incoming_slot >= 0
    safe_slot = jnp.maximum(incoming_slot, 0)
    spread_back = jax.vmap(pick_rows)(lifted, pool_group)
    h_out = (h_cells.astype(jnp.float32) + spread_back).astype(jnp.bfloat16)
    returning = jnp.where(
        sent_back[:, None, None], jnp.take(h_out, safe_slot, axis=0), jnp.zeros((), jnp.bfloat16)
    )
    returned = lax.all_to_all(returning, "gy", split_axis=0, concat_axis=0, tiled=True)
    return jnp.where(
        live_z[:, None, None], jnp.take(returned, position, axis=0), jnp.zeros((), jnp.bfloat16)
    )


def solution(mesh):
    in_specs = (
        P(("gx", "gy"), None, None),
        P(("gx", "gy")),
        P(("gx", "gy")),
        P(("gx", "gy"), None),
        P(),
        P(),
        P(),
        P(),
        P(),
        P(),
        P(),
        P(),
        P(),
        P(),
        P(),
        P(),
        P(),
    )
    out_specs = P(("gx", "gy"), None, None)
    return jax.shard_map(shards, mesh=mesh, in_specs=in_specs, out_specs=out_specs, check_vma=False)
```

profile of v0, /device:TPU:0, one launch (start us, length us, event | category | flops | bytes accessed | tf_op | source)
XLA Modules:
  0.0 691.5 jit_solution(17682398203502526985)
XLA Ops:
  5.5 7.3 %all-to-all-start.2 = ((s32[8,8,1]{1,2,0:T(1,128)}), s32[8,8,1]{1,2,0:T(1,128)}, u32[]{:S(2)}, u32[]{:S(2)}) async-start(s32[8,8,1]{1,2,0:T(1,128)} %bitcast.36), calls=%async_computation.2 | async-start | bytes 8192 | tf_op jit(solution)/shard_map/all_to_all | solution.py:148
  33.1 4.7 copy.57
  37.8 6.2 reshape.314
  43.9 4.6 copy.58
  48.6 157.5 %while.2 = (s32[]{:T(128)}, bf16[4,1024,8,16]{1,3,2,0:T(8,128)(2,1)S(1)}, bf16[4,1024,3,8,16]{1,4,3,2,0:T(8,128)(2,1)}, pred[4,1024]{1,0:T(4,128)(4,1)S(1)}, s32[]{:T(128)}) while((s32[]{:T(128)}, bf16[4,1024,8,16]{1,3,2,0:T(8,128)(2,1)S(1)}, bf16[4,1024,3,8,16]{1,4,3,2,0:T(8,128)(2,1)}, pred[4,1024]{1,0:T(4,128)(4,1)S(1)}, s32[]{:T(128)}) %tuple.72), condition=%wide.region_14.15_spmd, body=%wide.region_5.14_spmd.sunk | while | flops 588386304 | bytes 72423504 | solution.py:74
  50.0 4.9 fusion.599
  54.9 4.6 fusion.600
  59.5 4.9 fusion.597
  64.4 4.6 fusion.598
  69.0 4.9 fusion.595
  73.9 4.6 fusion.596
  78.5 4.9 fusion.593
  83.4 4.6 fusion.594
  89.4 4.9 fusion.599
  94.2 4.6 fusion.600
  98.9 4.9 fusion.597
  103.7 4.6 fusion.598
  108.4 4.9 fusion.595
  113.2 4.6 fusion.596
  117.9 4.9 fusion.593
  122.7 4.6 fusion.594
  128.7 4.9 fusion.599
  133.6 4.6 fusion.600
  138.2 4.9 fusion.597
  147.7 4.9 fusion.595
  152.5 4.6 fusion.596
  157.2 4.9 fusion.593
  162.0 4.6 fusion.594
  168.0 4.9 fusion.599
  172.9 4.6 fusion.600
  177.5 4.9 fusion.597
  182.4 4.6 fusion.598
  187.0 4.9 fusion.595
  191.9 4.6 fusion.596
  196.5 4.9 fusion.593
  201.4 4.6 fusion.594
  210.1 20.6 %fusion.119 = bf16[4096,128]{1,0:T(8,128)(2,1)} fusion(f32[4096,128]{1,0:T(8,128)S(1)} %get-tuple-element.113, bf16[512,128]{1,0:T(8,128)(2,1)S(1)} %copy-done.60, bf16[128,512]{1,0:T(8,128)(2,1)S(1)} %copy-done.61, f32[128]{0:T(128)S(1)} %copy-done.58, f32[4096]{0:T(1024)S(1)} %add_rsqrt_fusion.1, f32[4096]{0:T(1024)S(1)} %broadcast_multiply_fusion.1), kind=kOutput, calls=%fused_computation.155 | convolution fusion | flops 1213202432 | bytes 3441152 | tf_op jit(solution)/shard_map/dot_general | solution.py:80
  235.7 6.0 all-to-all-start
  242.4 5.7 all-to-all-done
  261.9 37.4 %all-to-all-done.1 = bf16[64,128,128]{2,1,0:T(8,128)(2,1)} async-done(((bf16[64,128,128]{2,1,0:T(8,128)(2,1)}), bf16[64,128,128]{2,1,0:T(8,128)(2,1)}, u32[]{:S(2)}, u32[]{:S(2)}) %all-to-all-start.1) | async-done | bytes 2097184 | tf_op jit(solution)/shard_map/all_to_all | solution.py:146
  304.4 9.9 %slice.394 = f32[32,63,256]{2,1,0:T(8,128)} slice(f32[32,128,256]{2,1,0:T(8,128)} %copy-done.4), slice={[0:32:1], [2:128:2], [0:256:1]} | slice | bytes 4128768 | tf_op jit(solution)/shard_map/slice | solution.py:162
  314.2 9.8 %slice.355 = f32[32,64,256]{2,1,0:T(8,128)} slice(f32[32,128,256]{2,1,0:T(8,128)} %copy-done.4), slice={[0:32:1], [1:128:2], [0:256:1]} | slice | bytes 4194304 | tf_op jit(solution)/shard_map/slice | solution.py:162
  324.0 9.8 %slice.354 = f32[32,64,256]{2,1,0:T(8,128)} slice(f32[32,128,256]{2,1,0:T(8,128)} %copy-done.4), slice={[0:32:1], [0:127:2], [0:256:1]} | slice | bytes 4194304 | tf_op jit(solution)/shard_map/slice | solution.py:162
  360.8 12.5 %pad.101 = f32[32,64,256]{2,1,0:T(8,128)S(1)} pad(f32[32,32,256]{2,1,0:T(8,128)} %pad_maximum_fusion.1, f32[]{:T(128)} %constant.91.clone.1), padding=0_0_0x0_1_1x0_0_0 | pad | bytes 3145732 | tf_op jit(solution)/shard_map/pad | solution.py:162
  373.2 16.9 %pad.102 = f32[32,64,256]{2,1,0:T(8,128)} pad(f32[32,32,256]{2,1,0:T(8,128)} %add.271, f32[]{:T(128)} %constant.91.clone.1), padding=0_0_0x1_0_1x0_0_0 | pad | bytes 3145732 | tf_op jit(solution)/shard_map/pad | solution.py:162
  395.6 19.1 %pad.103 = f32[32,128,256]{2,1,0:T(8,128)} pad(f32[32,64,256]{2,1,0:T(8,128)} %pad_maximum_fusion, f32[]{:T(128)} %constant.91.clone.1), padding=0_0_0x0_1_1x0_0_0 | pad | bytes 6291460 | tf_op jit(solution)/shard_map/pad | solution.py:162
  414.7 12.7 %pad.104 = f32[32,128,256]{2,1,0:T(8,128)} pad(f32[32,64,256]{2,1,0:T(8,128)S(1)} %copy-done.10, f32[]{:T(128)} %constant.91.clone.1), padding=0_0_0x1_0_1x0_0_0 | pad | bytes 6291460 | tf_op jit(solution)/shard_map/pad | solution.py:162
  427.4 6.1 add.273
  433.6 11.8 %gather_fusion.3 = f32[1024,256]{1,0:T(8,128)S(1)} fusion(f32[32,128,256]{2,1,0:T(8,128)} %add.273, s32[1024]{0:T(1024)S(1)} %reshape.376), kind=kCustom, calls=%fused_computation.7 | custom fusion | bytes 2105344 | tf_op jit(solution)/shard_map/vmap()/gather | solution.py:91
  446.0 37.7 %all-reduce.26 = (f32[256]{0:T(256)S(1)}, f32[]{:T(128)}, f32[256]{0:T(256)S(1)}) all-reduce(f32[256]{0:T(256)S(1)} %get-tuple-element.59, f32[]{:T(128)S(6)} %mul.269, f32[256]{0:T(256)S(1)} %get-tuple-element.58), channel_id=1, replica_groups=mesh['gx'=4,'gy'=8] {'gx','gy'}, use_global_device_ids=true, to_apply=%region_20.23 | all-reduce | flops 513 | bytes 4104 | tf_op jit(solution)/shard_map/psum | solution.py:177
  493.6 6.7 fusion.544
  500.3 6.7 fusion.535
  507.0 6.7 fusion.526
  513.6 6.7 fusion.517
  520.3 6.8 fusion.508
  527.1 6.7 fusion.499
  533.8 6.7 fusion.490
  540.5 6.7 fusion.481
  547.2 4.8 fusion.186
  552.0 4.8 fusion.187
  571.4 10.3 %fusion.175 = bf16[1024,256]{0,1:T(8,128)(2,1)S(1)} fusion(f32[1024,256]{0,1:T(8,128)S(1)} %get-tuple-element.131, bf16[1024,256]{1,0:T(8,128)(2,1)S(1)} %copy-done, bf16[256,1024]{1,0:T(8,128)(2,1)S(1)} %copy-done.59, f32[256]{0:T(256)S(1)} %bitcast.209, f32[1024]{0:T(1024)S(1)} %add_rsqrt_fusion.2, f32[1024]{0:T(1024)S(1)} %broadcast_multiply_fusion.3), kind=kOutput, calls=%fused_computation.235 | convolution fusion | flops 1143472128 | bytes 2630656 | tf_op jit(solution)/shard_map/dot_general | solution.py:80
  582.1 44.4 %gather_fusion.4 = f32[4096,128]{1,0:T(8,128)} fusion(f32[32,32,128]{2,1,0:T(8,128)S(1)} %bitcast.187, s32[4096]{0:T(1024)S(1)} %copy-done.3), kind=kCustom, calls=%fused_computation.8 | custom fusion | bytes 4227072 | tf_op jit(solution)/shard_map/vmap()/gather | solution.py:91
  634.0 6.3 all-to-all-start.3
  640.4 46.6 %all-to-all-done.3 = bf16[64,128,128]{2,1,0:T(8,128)(2,1)S(1)} async-done(((bf16[64,128,128]{2,1,0:T(8,128)(2,1)}), bf16[64,128,128]{2,1,0:T(8,128)(2,1)S(1)}, u32[]{:S(2)}, u32[]{:S(2)}) %all-to-all-start.3) | async-done | bytes 2097184 | tf_op jit(solution)/shard_map/all_to_all | solution.py:199
  (383 shorter events, 131.2 us)
Async XLA Ops:
  0.0 570.9 %copy-start = (bf16[1024,256]{1,0:T(8,128)(2,1)S(1)}, bf16[1024,256]{1,0:T(8,128)(2,1)}, u32[]{:S(2)}) copy-start(bf16[1024,256]{1,0:T(8,128)(2,1)} %param.37) | copy-start | bytes 1572868
  0.0 29.1 %copy-start.6 = (bf16[32,128,128]{2,1,0:T(8,128)(2,1)S(1)}, bf16[32,128,128]{2,1,0:T(8,128)(2,1)}, u32[]{:S(2)}) copy-start(bf16[32,128,128]{2,1,0:T(8,128)(2,1)} %param.23) | copy-start | bytes 3145732
  0.0 30.4 %copy-start.24 = (bf16[128,384]{1,0:T(8,128)(2,1)S(1)}, bf16[128,384]{1,0:T(8,128)(2,1)}, u32[]{:S(2)}) copy-start(bf16[128,384]{1,0:T(8,128)(2,1)} %param.27) | copy-start | bytes 294916
  2.2 30.9 %copy-start.1 = (pred[32]{0:T(512)(128)(4,1)}, pred[32]{0:T(512)(128)(4,1)S(1)}, u32[]{:S(2)}) copy-start(pred[32]{0:T(512)(128)(4,1)S(1)} %get-tuple-element.132) | copy-start | bytes 100
  2.7 10.6 %copy-start.42 = (pred[64]{0:T(512)(128)(4,1)}, pred[64]{0:T(512)(128)(4,1)S(1)}, u32[]{:S(2)}) copy-start(pred[64]{0:T(512)(128)(4,1)S(1)} %fusion.352) | copy-start | bytes 196
  5.5 230.2 %all-to-all-start.2 = ((s32[8,8,1]{1,2,0:T(1,128)}), s32[8,8,1]{1,2,0:T(1,128)}, u32[]{:S(2)}, u32[]{:S(2)}) async-start(s32[8,8,1]{1,2,0:T(1,128)} %bitcast.36), calls=%async_computation.2 | async-start | bytes 8192 | tf_op jit(solution)/shard_map/all_to_all | solution.py:148
  15.4 17.6 %copy-start.13 = (s32[32,128]{0,1:T(8,128)}, s32[32,128]{0,1:T(8,128)S(1)}, u32[]{:S(2)}) copy-start(s32[32,128]{0,1:T(8,128)S(1)} %copy.60) | copy-start | bytes 49156
  15.5 17.6 %copy-start.15 = (s32[32,64,1]{0,1,2:T(8,128)}, s32[32,64,1]{0,1,2:T(8,128)S(1)}, u32[]{:S(2)}) copy-start(s32[32,64,1]{0,1,2:T(8,128)S(1)} %slice.333) | copy-start | bytes 24580
  15.5 17.6 %copy-start.18 = (s32[32,32,1]{0,1,2:T(8,128)}, s32[32,32,1]{0,1,2:T(8,128)S(1)}, u32[]{:S(2)}) copy-start(s32[32,32,1]{0,1,2:T(8,128)S(1)} %slice.336) | copy-start | bytes 12292
  16.0 17.0 %copy-start.22 = (s32[32,16,1]{0,1,2:T(8,128)}, s32[32,16,1]{0,1,2:T(8,128)S(1)}, u32[]{:S(2)}) copy-start(s32[32,16,1]{0,1,2:T(8,128)S(1)} %slice.339) | copy-start | bytes 6148
  16.1 17.0 %copy-start.32 = (s32[32,4,1]{0,1,2:T(4,128)}, s32[32,4,1]{0,1,2:T(4,128)S(1)}, u32[]{:S(2)}) copy-start(s32[32,4,1]{0,1,2:T(4,128)S(1)} %slice.345) | copy-start | bytes 1540
  16.1 17.0 %copy-start.33 = (s32[32,2,1]{0,1,2:T(2,128)}, s32[32,2,1]{0,1,2:T(2,128)S(1)}, u32[]{:S(2)}) copy-start(s32[32,2,1]{0,1,2:T(2,128)S(1)} %slice.348) | copy-start | bytes 772
  206.9 3.1 copy-start.27
  206.9 3.1 copy-start.55
  206.9 3.1 copy-start.25
  206.9 3.1 copy-start.26
  206.9 3.1 copy-start.58
  207.0 3.1 copy-start.60
  207.0 3.1 copy-start.61
  230.7 4.2 copy-start.16
  230.7 4.2 copy-start.19
  230.7 4.2 copy-start.14
  230.7 4.3 copy-start.44
  230.7 10.9 %copy-start.30 = (s32[32,32,1]{1,0,2:T(8,128)S(1)}, s32[32,32,1]{1,0,2:T(8,128)}, u32[]{:S(2)}) copy-start(s32[32,32,1]{1,0,2:T(8,128)} %fusion.346) | copy-start | bytes 12292
  230.8 11.0 %copy-start.47 = (pred[32,4]{0,1:T(4,128)(4,1)S(1)}, pred[32,4]{0,1:T(4,128)(4,1)}, u32[]{:S(2)}) copy-start(pred[32,4]{0,1:T(4,128)(4,1)} %compare_bitcast_fusion.7) | copy-start | bytes 388
  230.8 11.1 %copy-start.46 = (pred[32,3]{0,1:T(4,128)(4,1)S(1)}, pred[32,3]{0,1:T(4,128)(4,1)}, u32[]{:S(2)}) copy-start(pred[32,3]{0,1:T(4,128)(4,1)} %fusion.357) | copy-start | bytes 292
  230.8 11.2 %copy-start.45 = (pred[32,2]{0,1:T(4,128)(4,1)S(1)}, pred[32,2]{0,1:T(4,128)(4,1)}, u32[]{:S(2)}) copy-start(pred[32,2]{0,1:T(4,128)(4,1)} %compare_bitcast_fusion.5) | copy-start | bytes 196
  230.8 11.3 %copy-start.37 = (pred[32,7]{0,1:T(8,128)(4,1)S(1)}, pred[32,7]{0,1:T(8,128)(4,1)}, u32[]{:S(2)}) copy-start(pred[32,7]{0,1:T(8,128)(4,1)} %fusion.356) | copy-start | bytes 676
  230.8 11.4 %copy-start.38 = (pred[32,8]{0,1:T(8,128)(4,1)S(1)}, pred[32,8]{0,1:T(8,128)(4,1)}, u32[]{:S(2)}) copy-start(pred[32,8]{0,1:T(8,128)(4,1)} %compare_bitcast_fusion.3) | copy-start | bytes 772
  233.2 19.6 %copy-start.23 = (s32[32,16,1]{0,1,2:T(8,128)S(1)}, s32[32,16,1]{0,1,2:T(8,128)}, u32[]{:S(2)}) copy-start(s32[32,16,1]{0,1,2:T(8,128)} %copy-done.22) | copy-start | bytes 6148
  233.2 20.1 %copy-start.34 = (s32[32,2,1]{0,1,2:T(2,128)S(1)}, s32[32,2,1]{0,1,2:T(2,128)}, u32[]{:S(2)}) copy-start(s32[32,2,1]{0,1,2:T(2,128)} %copy-done.33) | copy-start | bytes 772
  233.2 20.1 %copy-start.40 = (s32[32,2,1]{0,1,2:T(2,128)S(1)}, s32[32,2,1]{0,1,2:T(2,128)}, u32[]{:S(2)}) copy-start(s32[32,2,1]{0,1,2:T(2,128)} %copy-done.39) | copy-start | bytes 772
  233.2 20.8 %copy-start.48 = (f32[2,256]{1,0:T(2,128)S(1)}, f32[2,256]{1,0:T(2,128)}, u32[]{:S(2)}) copy-start(f32[2,256]{1,0:T(2,128)} %param.38) | copy-start | bytes 6148
  233.2 21.4 %copy-start.20 = (s32[32,128]{1,0:T(8,128)S(1)}, s32[32,128]{1,0:T(8,128)}, u32[]{:S(2)}) copy-start(s32[32,128]{1,0:T(8,128)} %param.26) | copy-start | bytes 49156
  234.9 66.8 %copy-start.28 = (bf16[128,256]{1,0:T(8,128)(2,1)S(1)}, bf16[128,256]{1,0:T(8,128)(2,1)}, u32[]{:S(2)}) copy-start(bf16[128,256]{1,0:T(8,128)(2,1)} %param.32) | copy-start | bytes 196612
  235.7 12.4 %all-to-all-start = ((s32[8,8,1]{1,2,0:T(1,128)}), s32[8,8,1]{1,2,0:T(1,128)S(1)}, u32[]{:S(2)}, u32[]{:S(2)}) async-start(s32[8,8,1]{1,2,0:T(1,128)} %bitcast.12), calls=%async_computation | async-start | bytes 8192 | tf_op jit(solution)/shard_map/all_to_all | solution.py:147
  248.1 51.2 %all-to-all-start.1 = ((bf16[64,128,128]{2,1,0:T(8,128)(2,1)}), bf16[64,128,128]{2,1,0:T(8,128)(2,1)}, u32[]{:S(2)}, u32[]{:S(2)}) async-start(bf16[64,128,128]{2,1,0:T(8,128)(2,1)} %select_select_fusion.1), calls=%async_computation.1 | async-start | bytes 4194304 | tf_op jit(solution)/shard_map/all_to_all | solution.py:146
  259.3 54.9 %copy-start.35 = (pred[32]{0:T(512)(128)(4,1)}, pred[32]{0:T(512)(128)(4,1)S(1)}, u32[]{:S(2)}) copy-start(pred[32]{0:T(512)(128)(4,1)S(1)} %get-tuple-element.79) | copy-start | bytes 100
  301.6 12.6 %copy-start.8 = (bf16[32,128,128]{2,1,0:T(8,128)(2,1)}, bf16[32,128,128]{2,1,0:T(8,128)(2,1)S(1)}, u32[]{:S(2)}) copy-start(bf16[32,128,128]{2,1,0:T(8,128)(2,1)S(1)} %gather_fusion.6) | copy-start | bytes 3145732
  353.4 2.7 copy-start.12
  390.1 3.4 copy-start.5
  390.1 3.4 copy-start.11
  395.6 19.1 %copy-start.10 = (f32[32,64,256]{2,1,0:T(8,128)S(1)}, f32[32,64,256]{2,1,0:T(8,128)}, u32[]{:S(2)}) copy-start(f32[32,64,256]{2,1,0:T(8,128)} %add.272) | copy-start | bytes 6291460
  433.6 50.7 %copy-start.41 = (f32[256]{0:T(256)S(1)}, f32[256]{0:T(256)}, u32[]{:S(2)}) copy-start(f32[256]{0:T(256)} %param.33) | copy-start | bytes 3076
  445.3 46.0 %copy-start.17 = (bf16[256,768]{1,0:T(8,128)(2,1)S(1)}, bf16[256,768]{1,0:T(8,128)(2,1)}, u32[]{:S(2)}) copy-start(bf16[256,768]{1,0:T(8,128)(2,1)} %param.34) | copy-start | bytes 1179652
  493.6 6.7 copy-start.50
  547.2 9.6 %slice-start.10 = ((s8[8388608]{0:T(1024)(128)(4,1)}), s8[4194304]{0:T(1024)(128)(4,1)S(1)}, s32[]{:S(2)}) async-start(s8[8388608]{0:T(1024)(128)(4,1)} %bitcast.220), calls=%async_computation.14 | async-start | bytes 8388608
  552.0 4.8 slice-start.11
  552.0 6.3 slice-start.8
  556.8 2.5 slice-start.9
  556.8 3.7 slice-start.6
  559.3 3.7 slice-start.4
  561.7 3.7 slice-start.2
  564.2 3.7 slice-start
  571.4 10.3 %copy-start.29 = (bf16[256,128]{1,0:T(8,128)(2,1)S(1)}, bf16[256,128]{1,0:T(8,128)(2,1)}, u32[]{:S(2)}) copy-start(bf16[256,128]{1,0:T(8,128)(2,1)} %param.39) | copy-start | bytes 196612
  571.4 10.7 %copy-start.3 = (s32[4096]{0:T(1024)S(1)}, s32[4096]{0:T(1024)}, u32[]{:S(2)}) copy-start(s32[4096]{0:T(1024)} %fusion.351) | copy-start | bytes 49156
  582.1 44.5 %copy-start.9 = (bf16[32,128,128]{2,1,0:T(8,128)(2,1)S(1)}, bf16[32,128,128]{2,1,0:T(8,128)(2,1)}, u32[]{:S(2)}) copy-start(bf16[32,128,128]{2,1,0:T(8,128)(2,1)} %copy-done.8) | copy-start | bytes 3145732
  582.1 44.4 %copy-start.36 = (pred[32]{0:T(512)(128)(4,1)S(1)}, pred[32]{0:T(512)(128)(4,1)}, u32[]{:S(2)}) copy-start(pred[32]{0:T(512)(128)(4,1)} %copy-done.35) | copy-start | bytes 100
  626.5 4.2 copy-start.52
  626.5 4.2 copy-start.53
  630.8 9.6 %copy-start.57 = (s32[32]{0:T(128)S(1)}, s32[32]{0:T(128)}, u32[]{:S(2)}) copy-start(s32[32]{0:T(128)} %copy-done.56) | copy-start | bytes 388
  634.0 54.6 %copy-start.2 = (pred[32]{0:T(512)(128)(4,1)S(1)}, pred[32]{0:T(512)(128)(4,1)}, u32[]{:S(2)}) copy-start(pred[32]{0:T(512)(128)(4,1)} %copy-done.1) | copy-start | bytes 100
  634.0 54.6 %copy-start.49 = (pred[32]{0:T(512)(128)(4,1)S(1)}, pred[32]{0:T(512)(128)(4,1)}, u32[]{:S(2)}) copy-start(pred[32]{0:T(512)(128)(4,1)} %get-tuple-element.71) | copy-start | bytes 100
  634.0 53.0 %all-to-all-start.3 = ((bf16[64,128,128]{2,1,0:T(8,128)(2,1)}), bf16[64,128,128]{2,1,0:T(8,128)(2,1)S(1)}, u32[]{:S(2)}, u32[]{:S(2)}) async-start(bf16[64,128,128]{2,1,0:T(8,128)(2,1)} %select_select_fusion), calls=%async_computation.3 | async-start | bytes 4194304 | tf_op jit(solution)/shard_map/all_to_all | solution.py:199
  (14 other events, 23.3 us)
where the time goes:
time: 703 us; the launch traced here: 691 us
  matrix products  260 us (37%)
  local copies, waits for them, and re-layouts  218 us (31%)
  waiting for transfers between devices  89.8 us (13%)
  other arithmetic  58.7 us (8%)
  blocking collectives  37.7 us (5%)
  starting transfers between devices  24.2 us (3%)
    sub x24, matrix products, attend_patch(): exponent = jnp.exp(scores - row_max)  131 us
    dot_general x24, matrix products, attend_patch(): jnp.einsum('hqk,khd->qhd', weights, values[:, head_start:head_start + hea...  91.5 us
    pad x20, local copies, waits for them, and re-layouts, shards(): lax.associative_scan(running_max, (y_cells, pool_group[:, :, None]), axis=1)  66 us
    gather x4, local copies, waits for them, and re-layouts, pick_rows(): return cell_rows[row_index]  56.6 us
    all_to_all x1, waiting for transfers between devices, shards(): lax.all_to_all(returning, 'gy', split_axis=0, concat_axis=0, tiled=True)  46.6 us
    slice x46, local copies, waits for them, and re-layouts, shards(): lax.associative_scan(running_max, (y_cells, pool_group[:, :, None]), axis=1)  45.6 us
    psum x1, blocking collectives, shards(): lax.psum((local_sum, local_square, local_count), ('gx', 'gy'))  37.7 us
    all_to_all x1, waiting for transfers between devices, shards(): lax.all_to_all(outgoing, 'gy', split_axis=0, concat_axis=0, tiled=True)  37.4 us
  transfers between devices with their start and end apart: 4, of which 3 were waited for; matrix products, arithmetic and copies ran while one was open for 33% of the time, Pallas kernels for 0%

commit v1 on v0

v1 whole, which is shorter than its diff:
```python
import functools

import jax
import jax.numpy as jnp
from jax import lax
from jax.experimental import pallas as pl
from jax.experimental.pallas import tpu as pltpu
from jax.sharding import PartitionSpec as P

HEAD = 16
PGROUP = 32
PATCH = 1024
MOSTG = 8
LANES = 128
ROWS = 256
QROWS = 512
UNROLL = 2

EPSILON = 1e-05
MASKED = -1e30
BF = jnp.bfloat16
F32 = jnp.float32
VMEM = pl.BlockSpec(memory_space=pltpu.VMEM)
SMEM = pl.BlockSpec(memory_space=pltpu.SMEM)


def dot(a, b):
    return jnp.dot(a, b, preferred_element_type=F32)


def gelu(values):
    return 0.5 * values * (1.0 + lax.erf(values * (0.5**0.5)))


def normed(values, gain):
    average = jnp.mean(values, axis=-1, keepdims=True)
    centred = values - average
    spread = jnp.mean(centred * centred, axis=-1, keepdims=True)
    return (centred * lax.rsqrt(spread + EPSILON) * gain).astype(BF)


def lane_ids(rows):
    return lax.broadcasted_iota(jnp.int32, (rows, LANES), 1)


def attend(q_ref, k_ref, v_ref, att_ref):
    patch_rows = q_ref.shape[0]
    first_lane = (lane_ids(QROWS) == 0).astype(F32).astype(BF)
    blocks = patch_rows // QROWS

    def head_step(head, _):
        own = lane_ids(QROWS) // HEAD == head
        for block in range(blocks):
            rows = pl.ds(block * QROWS, QROWS)
            picked = jnp.where(own, q_ref[rows, :].astype(F32), 0.0).astype(BF)
            queries = jnp.concatenate([picked, first_lane], axis=1)
            scores = lax.dot_general(
                queries, k_ref[...], (((1,), (1,)), ((), ())), preferred_element_type=F32
            )
            top = jnp.max(scores, axis=-1, keepdims=True)
            weights = jnp.exp(scores - top).astype(BF)
            mixed = dot(weights, v_ref[...])
            att_ref[rows, :] = jnp.where(own, mixed[:, :LANES] / mixed[:, LANES:], att_ref[rows, :])
        return 0

    lax.fori_loop(0, LANES // HEAD, head_step, 0, unroll=UNROLL)


def block_body(
    load_rows, store_rows, bias_of, unit_rows, width, gain_ref, qkv_ref, proj_ref, up_ref, down_ref,
    q_scr, k_scr, v_scr, att_scr,
):
    slices = width // LANES
    chunks = PATCH // ROWS

    def project(chunk, _):
        rows = pl.ds(pl.multiple_of(chunk * ROWS, ROWS), ROWS)
        normal = normed(load_rows(chunk).astype(F32), gain_ref[0:1, :])
        packed = dot(normal, qkv_ref[...])
        for part in range(slices):
            start = part * LANES
            q_scr[part, rows, :] = (packed[:, start : start + LANES].astype(BF).astype(F32) * HEAD**-0.5).astype(BF)
            k_scr[part, rows, 0:LANES] = packed[:, width + start : width + start + LANES].astype(BF)
            v_scr[part, rows, 0:LANES] = packed[:, 2 * width + start : 2 * width + start + LANES].astype(BF)
            v_scr[part, rows, LANES:] = jnp.ones((ROWS, LANES), BF)
        return 0

    lax.fori_loop(0, chunks, project, 0)

    def mask_unit(unit, _):
        rows = pl.ds(pl.multiple_of(unit * unit_rows, unit_rows), unit_rows)
        bias = jnp.where(lane_ids(unit_rows) == 0, bias_of(unit), 0.0).astype(BF)
        for part in range(slices):
            k_scr[part, rows, LANES:] = bias
        return 0

    lax.fori_loop(0, PATCH // unit_rows, mask_unit, 0)

    for part in range(slices):
        attend(q_scr.at[part], k_scr.at[part], v_scr.at[part], att_scr.at[part])

    def finish(chunk, _):
        rows = pl.ds(pl.multiple_of(chunk * ROWS, ROWS), ROWS)
        attended = jnp.concatenate([att_scr[part, rows, :] for part in range(slices)], axis=1).astype(BF)
        middle = load_rows(chunk).astype(F32) + dot(attended, proj_ref[...])
        normal = normed(middle, gain_ref[1:2, :])
        hidden = gelu(dot(normal, up_ref[...])).astype(BF)
        store_rows(chunk, (middle + dot(hidden, down_ref[...])).astype(BF))
        return 0

    lax.fori_loop(0, chunks, finish, 0)


def block_scratch(width):
    slices = width // LANES
    return [
        pltpu.VMEM((slices, PATCH, LANES), BF),
        pltpu.VMEM((slices, PATCH, 2 * LANES), BF),
        pltpu.VMEM((slices, PATCH, 2 * LANES), BF),
        pltpu.VMEM((slices, PATCH, LANES), F32),
    ]


def params(**more):
    return pltpu.CompilerParams(vmem_limit_bytes=48 * 2**20, **more)


def block_cost(rows, width):
    flops = 2 * rows * (12 * width * width) + 4 * rows * PATCH * 256 * (width // HEAD)
    return pl.CostEstimate(
        flops=flops, bytes_accessed=4 * rows * width, transcendentals=rows * PATCH * (width // HEAD)
    )


def z_kernel(cell_points, count_ref, x_ref, gain, qkv, proj, up, down, out_ref, *scratch):
    first_cell = pl.program_id(0) * (PATCH // cell_points)

    def load_rows(chunk):
        return x_ref[pl.ds(pl.multiple_of(chunk * ROWS, ROWS), ROWS), :]

    def store_rows(chunk, rows):
        out_ref[pl.ds(pl.multiple_of(chunk * ROWS, ROWS), ROWS), :] = rows

    def bias_of(unit):
        return jnp.where(first_cell + unit < count_ref[0], 0.0, MASKED)

    block_body(load_rows, store_rows, bias_of, cell_points, x_ref.shape[1], gain, qkv, proj, up, down, *scratch)


def z_block(rows, z_count, cell_points, gain, qkv, proj, up, down):
    count, width = rows.shape
    return pl.pallas_call(
        functools.partial(z_kernel, cell_points),
        grid=(count // PATCH,),
        in_specs=[SMEM, pl.BlockSpec((PATCH, width), lambda i: (i, 0))] + [VMEM] * 5,
        out_specs=pl.BlockSpec((PATCH, width), lambda i: (i, 0)),
        out_shape=jax.ShapeDtypeStruct((count, width), BF),
        scratch_shapes=block_scratch(width),
        compiler_params=params(),
        cost_estimate=block_cost(count, width),
        name="z_block",
    )(z_count, rows, gain, qkv, proj, up, down)


def pool_kernel(count_ref, z_ref, group_ref, pool_ref, out_ref, stat_ref):
    cells, points, _ = z_ref.shape
    width = pool_ref.shape[1]
    groups = lax.broadcasted_iota(jnp.int32, (PGROUP, points), 0)
    lanes = lax.broadcasted_iota(jnp.int32, (PGROUP, points), 1)

    def one(cell, carry):
        total, square = carry
        own = jnp.broadcast_to(group_ref[pl.ds(cell, 1), :], (PGROUP, points))
        start = jnp.sum((own < groups).astype(F32), axis=1, keepdims=True).astype(jnp.int32)
        last = jnp.sum((own <= groups).astype(F32), axis=1, keepdims=True).astype(jnp.int32) - 1
        picks = jnp.concatenate(
            [(lanes == jnp.minimum(start + j, last)).astype(F32) for j in range(MOSTG)], axis=0
        ).astype(BF)
        chosen = dot(picks, z_ref[cell]).astype(BF)
        y = dot(chosen, pool_ref[...])
        top = y[0:PGROUP]
        for j in range(1, MOSTG):
            top = jnp.maximum(top, y[j * PGROUP : (j + 1) * PGROUP])
        out_ref[cell] = top
        kept = jnp.where(cell < count_ref[0], top, 0.0)
        return total + kept, square + kept * kept

    zero = jnp.zeros((PGROUP, width), F32)
    total, square = lax.fori_loop(0, cells, one, (zero, zero), unroll=2)
    stat_ref[0:1, :] = jnp.sum(total, axis=0, keepdims=True)
    stat_ref[1:2, :] = jnp.sum(square, axis=0, keepdims=True)


def pool(z_out, z_count, group_z, pool_w):
    cells = z_out.shape[0]
    width = pool_w.shape[1]
    return pl.pallas_call(
        pool_kernel,
        in_specs=[SMEM, VMEM, VMEM, VMEM],
        out_specs=[VMEM, VMEM],
        out_shape=[
            jax.ShapeDtypeStruct((cells, PGROUP, width), F32),
            jax.ShapeDtypeStruct((2, width), F32),
        ],
        compiler_params=params(),
        name="pool",
    )(z_count, z_out, group_z, pool_w)


def bn_kernel(position_ref, top_ref, scale_ref, out_ref):
    average = scale_ref[0:1, :]
    spread = scale_ref[1:2, :]
    gain = scale_ref[2:3, :]

    def one(cell, _):
        out_ref[position_ref[cell]] = gelu((top_ref[cell] - average) * spread * gain).astype(BF)
        return 0

    lax.fori_loop(0, top_ref.shape[0], one, 0, unroll=2)


def batch_norm(top, position, scales, slots):
    return pl.pallas_call(
        bn_kernel,
        in_specs=[SMEM, VMEM, VMEM],
        out_specs=VMEM,
        out_shape=jax.ShapeDtypeStruct((slots,) + top.shape[1:], BF),
        compiler_params=params(),
        name="batch_norm",
    )(position, top, scales)


def p_kernel(anchor_ref, live_ref, in_ref, gain, qkv, proj, up, down, unpool, out_ref, *scratch):
    per_chunk = ROWS // PGROUP
    first_cell = pl.program_id(0) * (PATCH // PGROUP)

    def load_rows(chunk):
        return jnp.concatenate(
            [in_ref[anchor_ref[first_cell + chunk * per_chunk + i]] for i in range(per_chunk)], axis=0
        )

    def store_rows(chunk, rows):
        lifted = dot(rows, unpool[...]).astype(BF)
        for i in range(per_chunk):
            out_ref[anchor_ref[first_cell + chunk * per_chunk + i]] = lifted[i * PGROUP : (i + 1) * PGROUP]

    def bias_of(unit):
        return jnp.where(live_ref[first_cell + unit] > 0, 0.0, MASKED)

    block_body(load_rows, store_rows, bias_of, PGROUP, in_ref.shape[2], gain, qkv, proj, up, down, *scratch)


def p_block(incoming, anchor, live, gain, qkv, proj, up, down, unpool):
    slots, _, width = incoming.shape
    rows = anchor.shape[0] * PGROUP
    return pl.pallas_call(
        p_kernel,
        grid=(rows // PATCH,),
        in_specs=[SMEM, SMEM] + [VMEM] * 7,
        out_specs=VMEM,
        out_shape=jax.ShapeDtypeStruct((slots, PGROUP, unpool.shape[1]), BF),
        scratch_shapes=block_scratch(width),
        compiler_params=params(),
        cost_estimate=block_cost(rows, width),
        name="p_block",
    )(anchor, live, incoming, gain, qkv, proj, up, down, unpool)


def final_kernel(position_ref, count_ref, z_ref, group_ref, back_ref, out_ref):
    cells, points, _ = z_ref.shape
    groups = lax.broadcasted_iota(jnp.int32, (PGROUP, points), 0)

    def one(cell, _):
        own = jnp.broadcast_to(group_ref[pl.ds(cell, 1), :], (PGROUP, points))
        pick = (own == groups).astype(F32).astype(BF)
        lifted = lax.dot_general(
            pick, back_ref[position_ref[cell]], (((0,), (0,)), ((), ())), preferred_element_type=F32
        )
        result = z_ref[cell].astype(F32) + lifted
        out_ref[cell] = jnp.where(cell < count_ref[0], result, 0.0).astype(BF)
        return 0

    lax.fori_loop(0, cells, one, 0, unroll=2)


def final(position, z_count, z_out, group_z, returned):
    return pl.pallas_call(
        final_kernel,
        in_specs=[SMEM, SMEM, VMEM, VMEM, VMEM],
        out_specs=VMEM,
        out_shape=jax.ShapeDtypeStruct(z_out.shape, BF),
        compiler_params=params(),
        name="final",
    )(position, z_count, z_out, group_z, returned)


def shards(
    feats, z_count, hil_dest, pool_group,
    z_qkv, z_proj, z_up, z_down, z_gain,
    pool_w, bn_gain,
    p_qkv, p_proj, p_up, p_down, p_gain,
    unpool_w,
):
    cells, points, width = feats.shape
    row_devices = lax.axis_size("gy")
    me = lax.axis_index("gy")
    capacity = 2 * cells // row_devices
    slots = row_devices * capacity
    cell_ids = jnp.arange(cells, dtype=jnp.int32)

    head = jnp.zeros((8, points), jnp.int32)
    head = head.at[0, :cells].set(hil_dest).at[1, 0].set(z_count[0])
    everyone = lax.all_gather(jnp.concatenate([head, pool_group], axis=0), "gy", axis=0, tiled=False)
    all_dest = everyone[:, 0, :cells]
    all_count = everyone[:, 1, 0]
    group_all = everyone[:, 8:, :].reshape(row_devices * cells, points)
    group_z = jnp.take(group_all, hil_dest % (row_devices * cells), axis=0)

    target = hil_dest // cells % row_devices
    earlier = cell_ids[None, :] < cell_ids[:, None]
    rank = jnp.sum(((target[:, None] == target[None, :]) & earlier).astype(jnp.int32), axis=1)
    position = target * capacity + rank

    mine = all_dest // cells % row_devices == me
    arrival = jnp.sum((mine[:, None, :] & earlier[None]).astype(jnp.int32), axis=2)
    arrival = arrival + jnp.arange(row_devices, dtype=jnp.int32)[:, None] * capacity
    alive = (cell_ids[None, :] < all_count[:, None]).astype(jnp.int32)
    match = mine[None] & (all_dest[None] % cells == cell_ids[:, None, None])
    anchor = jnp.sum(jnp.where(match, arrival[None], 0), axis=(1, 2))
    live_h = jnp.sum(jnp.where(match, alive[None], 0), axis=(1, 2))

    z_out = z_block(
        feats.reshape(cells * points, width), z_count, points, z_gain, z_qkv, z_proj, z_up, z_down
    ).reshape(cells, points, width)

    top, stats = pool(z_out, z_count, group_z, pool_w)
    live = jnp.full((1, stats.shape[1]), z_count[0] * PGROUP, F32)
    stats = lax.psum(jnp.concatenate([stats, live], axis=0), ("gx", "gy"))
    average = stats[0] / stats[2]
    variance = stats[1] / stats[2] - average * average
    scales = jnp.stack([average, lax.rsqrt(variance + EPSILON), bn_gain])
    outgoing = batch_norm(top, position, scales, slots)
    incoming = lax.all_to_all(outgoing, "gy", split_axis=0, concat_axis=0, tiled=True)
    lifted = p_block(incoming, anchor, live_h, p_gain, p_qkv, p_proj, p_up, p_down, unpool_w)
    returned = lax.all_to_all(lifted, "gy", split_axis=0, concat_axis=0, tiled=True)
    return final(position, z_count, z_out, group_z, returned)


def solution(mesh):
    shard = ("gx", "gy")
    in_specs = (P(shard, None, None), P(shard), P(shard), P(shard, None)) + (P(),) * 13
    return jax.shard_map(
        shards, mesh=mesh, in_specs=in_specs, out_specs=P(shard, None, None), check_vma=False
    )
```

time: 703 us -> 239 us (0.34); the launches traced: 691 us -> 238 us
  matrix products: 260 us -> 0 us
  local copies, waits for them, and re-layouts: 218 us -> 4.56 us
  Pallas kernels: 0 us -> 112 us
  waiting for transfers between devices: 89.8 us -> 22.3 us
  other arithmetic: 58.7 us -> 2.71 us
  blocking collectives: 37.7 us -> 89.7 us
  starting transfers between devices: 24.2 us -> 6.05 us
    sub x24 -> x0, matrix products: 131 us -> none  [attend_patch(): exponent = jnp.exp(scores - row_max)]
    dot_general x32 -> x0, matrix products: 129 us -> none  [the longest x24 91.5 us: attend_patch(): jnp.einsum('hqk,khd->qhd', weights, values[:, head_start:head_start + hea...]
    pallas_call x0 -> x5, Pallas kernels: none -> 112 us  [the longest x1 67 us: z_block(): pl.pallas_call(functools.partial(z_kernel, cell_points), grid=(count // P...]
    gather x11 -> x1, local copies, waits for them, and re-layouts: 67.4 us -> 0.57 us  [shards(): group_z = jnp.take(group_all, hil_dest % (row_devices * cells), axis=0)]
    pad x20 -> x0, local copies, waits for them, and re-layouts: 66 us -> none  [shards(): lax.associative_scan(running_max, (y_cells, pool_group[:, :, None]), axis=1)]
    all_to_all x3 -> x0, waiting for transfers between devices: 52.4 us -> none  [the longest x1 46.6 us: shards(): lax.all_to_all(returning, 'gy', split_axis=0, concat_axis=0, tiled=True)]
    slice x47 -> x3, local copies, waits for them, and re-layouts: 46.2 us -> 0.25 us  [the longest x1 0.23 us: shards(): all_count = everyone[:, 1, 0]]
    all_gather x0 -> x1, blocking collectives: none -> 32.4 us  [shards(): lax.all_gather(jnp.concatenate([head, pool_group], axis=0), 'gy', axis=0,...]
  transfers between devices with their start and end apart: 4 -> 1, of which waited for: 3 -> 1; matrix products, arithmetic and copies ran while one was open for 33% -> 1% of each run, Pallas kernels for 0% -> 0%
where the time goes in v1:
time: 239 us; the launch traced here: 238 us
  Pallas kernels  112 us (47%)
  blocking collectives  89.7 us (38%)
  waiting for transfers between devices  22.3 us (9%)
  starting transfers between devices  6.05 us (3%)
  local copies, waits for them, and re-layouts  4.56 us (2%)
  other arithmetic  2.71 us (1%)
    pallas_call x1, Pallas kernels, z_block(): pl.pallas_call(functools.partial(z_kernel, cell_points), grid=(count // P...  67 us
    psum x1, blocking collectives, shards(): stats = lax.psum(jnp.concatenate([stats, live], axis=0), ('gx', 'gy'))  39.6 us
    all_gather x1, blocking collectives, shards(): lax.all_gather(jnp.concatenate([head, pool_group], axis=0), 'gy', axis=0,...  32.4 us
    pallas_call x1, Pallas kernels, p_block(): pl.pallas_call(p_kernel, grid=(rows // PATCH,), in_specs=[SMEM, SMEM] + [...  31.7 us
    all_to_all x1, waiting for transfers between devices, shards(): lax.all_to_all(outgoing, 'gy', split_axis=0, concat_axis=0, tiled=True)  22.3 us
    all_to_all x1, blocking collectives, shards(): lax.all_to_all(lifted, 'gy', split_axis=0, concat_axis=0, tiled=True)  17.7 us
    pallas_call x1, Pallas kernels, pool(): pl.pallas_call(pool_kernel, in_specs=[SMEM, VMEM, VMEM, VMEM], out_specs=...  6.77 us
    all_to_all x1, starting transfers between devices, shards(): lax.all_to_all(outgoing, 'gy', split_axis=0, concat_axis=0, tiled=True)  6.05 us
  transfers between devices with their start and end apart: 1, of which 1 were waited for; matrix products, arithmetic and copies ran while one was open for 1% of the time, Pallas kernels for 0%

profile of v1, /device:TPU:0, one launch (start us, length us, event | category | flops | bytes accessed | tf_op | source)
XLA Modules:
  0.0 238.4 jit_solution(14751511175272172713)
XLA Ops:
  0.0 0.0 copy-start.15
  0.0 0.0 copy-start.13
  0.0 0.7 and_select_fusion.3
  0.7 0.0 copy-done.15
  1.4 0.2 convert_reduce_fusion.1
  1.7 0.1 scatter.9
  1.7 0.0 copy-done.13
  1.8 32.4 %all-gather = s32[320,128]{1,0:T(8,128)S(1)} all-gather(s32[40,128]{1,0:T(8,128)S(1)} %pad_add_fusion), channel_id=2, replica_groups=mesh['gx'=4,'gy'=8] {'gy'}, dimensions={0}, use_global_device_ids=true | all-gather | bytes 184320 | tf_op jit(solution)/shard_map/all_gather | solution.py:313
  34.1 0.0 copy-start.6
  34.1 0.0 copy-start.8
  34.2 0.0 copy-start.5
  34.2 0.6 gather_fusion
  34.8 0.0 copy-start.10
  34.8 0.1 broadcast_select_fusion.group_ref
  34.8 0.0 copy-start.12
  34.8 0.2 copy-done.6
  35.1 0.1 copy-done.8
  35.1 0.1 copy-done.5
  35.2 0.4 copy-done.10
  35.6 0.0 copy-done.12
  35.6 0.0 copy-start.1
  35.6 1.2 copy-done.1
  36.8 0.0 copy-start
  36.8 67.0 %z_block.1 = bf16[4096,128]{1,0:T(8,128)(2,1)S(1)} custom-call(s32[1]{0:T(128)} %copy.24.count_ref, bf16[4096,128]{1,0:T(8,128)(2,1)S(1)} %bitcast.15, f32[2,128]{1,0:T(2,128)S(1)} %copy-done.12, bf16[128,384]{1,0:T(8,128)(2,1)S(1)} %copy-done.8, bf16[128,128]{1,0:T(8,128)(2,1)S(1)} %copy-done.10, bf16[128,512]{1,0:T(8,128)(2,1)S(1)} %copy-done.5, ...), custom_call_target="tpu_custom_call" | custom-call | flops 35970351104 | bytes 2097152 | tf_op jit(solution)/shard_map/z_block/pallas_call | solution.py:152
  103.8 0.0 copy-done
  103.8 6.8 %pool.1 = (f32[32,32,256]{2,1,0:T(8,128)S(1)}, f32[2,256]{1,0:T(2,128)S(1)}) custom-call(s32[1]{0:T(128)} %copy.24.count_ref, bf16[32,128,128]{2,1,0:T(8,128)(2,1)S(1)} %bitcast.13, s32[32,128]{1,0:T(8,128)S(1)} %broadcast_select_fusion.group_ref, bf16[128,256]{1,0:T(8,128)(2,1)S(1)} %copy-done), custom_call_target="tpu_custom_call" | custom-call | tf_op jit(solution)/shard_map/pool/pallas_call | solution.py:197
  110.6 39.6 %psum.7 = f32[3,256]{1,0:T(4,128)S(1)} all-reduce(f32[3,256]{1,0:T(4,128)S(1)} %concatenate.11), channel_id=1, replica_groups=mesh['gx'=4,'gy'=8] {'gx','gy'}, use_global_device_ids=true, to_apply=%region_4.5 | all-reduce | flops 768 | bytes 6144 | tf_op jit(solution)/shard_map/psum | solution.py:338
  150.3 0.0 copy-start.14
  150.3 0.7 copy-done.14
  151.0 1.9 batch_norm.1
  152.9 0.0 copy-start.2
  152.9 0.0 copy-start.3
  152.9 0.0 copy-start.7
  152.9 6.1 %all-to-all-start = ((bf16[64,32,256]{2,1,0:T(8,128)(2,1)}), bf16[64,32,256]{2,1,0:T(8,128)(2,1)S(1)}, u32[]{:S(2)}, u32[]{:S(2)}) async-start(bf16[64,32,256]{2,1,0:T(8,128)(2,1)} %batch_norm.1), calls=%async_computation | async-start | bytes 2097152 | tf_op jit(solution)/shard_map/all_to_all | solution.py:343
  158.9 0.0 copy-start.9
  159.0 0.2 slice_reduce_fusion
  159.3 0.2 convert_reduce_fusion
  159.5 0.1 fusion.2
  159.6 0.1 add_select_fusion
  159.7 1.2 select_reduce_fusion
  160.9 0.0 copy-start.11
  160.9 22.3 %all-to-all-done.in_ref = bf16[64,32,256]{2,1,0:T(8,128)(2,1)S(1)} async-done(((bf16[64,32,256]{2,1,0:T(8,128)(2,1)}), bf16[64,32,256]{2,1,0:T(8,128)(2,1)S(1)}, u32[]{:S(2)}, u32[]{:S(2)}) %all-to-all-start) | async-done | bytes 1048608 | tf_op jit(solution)/shard_map/all_to_all | solution.py:343
  183.2 0.0 copy-done.2
  183.2 0.0 copy-done.3
  183.2 0.0 copy-done.7
  183.2 0.0 copy-done.9
  183.2 0.0 copy-done.11
  183.2 0.0 copy-start.4
  183.2 1.0 copy-done.4
  184.2 31.7 %p_block.1 = bf16[64,32,128]{2,1,0:T(8,128)(2,1)S(1)} custom-call(s32[32]{0:T(128)S(1)} %get-tuple-element.34.anchor_ref, s32[32]{0:T(128)S(1)} %get-tuple-element.33.live_ref, bf16[64,32,256]{2,1,0:T(8,128)(2,1)S(1)} %all-to-all-done.in_ref, f32[2,256]{1,0:T(2,128)S(1)} %copy-done.11, bf16[256,768]{1,0:T(8,128)(2,1)S(1)} %copy-done.4, ...), custom_call_target="tpu_custom_call" | custom-call | flops 18790481920 | bytes 1048576 | tf_op jit(solution)/shard_map/p_block/pallas_call | solution.py:256
  215.9 17.7 %all_to_all.10.back_ref = bf16[64,32,128]{2,1,0:T(8,128)(2,1)S(1)} all-to-all(bf16[64,32,128]{2,1,0:T(8,128)(2,1)S(1)} %p_block.1), channel_id=1, replica_groups=mesh['gx'=4,'gy'=8] {'gy'}, dimensions={0} | all-to-all | bytes 1048576 | tf_op jit(solution)/shard_map/all_to_all | solution.py:345
  233.6 4.7 %final.1 = bf16[32,128,128]{2,1,0:T(8,128)(2,1)} custom-call(s32[32]{0:T(128)S(1)} %multiply_add_fusion.position_ref, s32[1]{0:T(128)} %copy.24.count_ref, bf16[32,128,128]{2,1,0:T(8,128)(2,1)S(1)} %bitcast.14, s32[32,128]{1,0:T(8,128)S(1)} %broadcast_select_fusion.group_ref, bf16[64,32,128]{2,1,0:T(8,128)(2,1)S(1)} %all_to_all.10.back_ref), custom_call_target="tpu_custom_call" | custom-call | tf_op jit(solution)/shard_map/final/pallas_call | solution.py:287
  (14 shorter events, 0.2 us)
Async XLA Ops:
  0.0 0.7 copy-start.15
  0.0 1.7 copy-start.13
  34.1 0.9 copy-start.6
  34.1 1.0 copy-start.8
  34.2 1.0 copy-start.5
  34.8 0.8 copy-start.10
  34.8 0.7 copy-start.12
  35.6 1.2 copy-start.1
  36.8 67.1 %copy-start = (bf16[128,256]{1,0:T(8,128)(2,1)S(1)}, bf16[128,256]{1,0:T(8,128)(2,1)}, u32[]{:S(2)}) copy-start(bf16[128,256]{1,0:T(8,128)(2,1)} %pool_ref.1) | copy-start | bytes 196612
  150.3 0.7 copy-start.14
  152.9 30.3 %copy-start.2 = (bf16[256,1024]{1,0:T(8,128)(2,1)S(1)}, bf16[256,1024]{1,0:T(8,128)(2,1)}, u32[]{:S(2)}) copy-start(bf16[256,1024]{1,0:T(8,128)(2,1)} %up.3) | copy-start | bytes 1572868
  152.9 30.3 %copy-start.3 = (bf16[1024,256]{1,0:T(8,128)(2,1)S(1)}, bf16[1024,256]{1,0:T(8,128)(2,1)}, u32[]{:S(2)}) copy-start(bf16[1024,256]{1,0:T(8,128)(2,1)} %down.3) | copy-start | bytes 1572868
  152.9 30.3 %copy-start.7 = (bf16[256,256]{1,0:T(8,128)(2,1)S(1)}, bf16[256,256]{1,0:T(8,128)(2,1)}, u32[]{:S(2)}) copy-start(bf16[256,256]{1,0:T(8,128)(2,1)} %proj.3) | copy-start | bytes 393220
  152.9 30.3 %all-to-all-start = ((bf16[64,32,256]{2,1,0:T(8,128)(2,1)}), bf16[64,32,256]{2,1,0:T(8,128)(2,1)S(1)}, u32[]{:S(2)}, u32[]{:S(2)}) async-start(bf16[64,32,256]{2,1,0:T(8,128)(2,1)} %batch_norm.1), calls=%async_computation | async-start | bytes 2097152 | tf_op jit(solution)/shard_map/all_to_all | solution.py:343
  158.9 24.3 %copy-start.9 = (bf16[256,128]{1,0:T(8,128)(2,1)S(1)}, bf16[256,128]{1,0:T(8,128)(2,1)}, u32[]{:S(2)}) copy-start(bf16[256,128]{1,0:T(8,128)(2,1)} %unpool.1) | copy-start | bytes 196612
  160.9 22.3 %copy-start.11 = (f32[2,256]{1,0:T(2,128)S(1)}, f32[2,256]{1,0:T(2,128)}, u32[]{:S(2)}) copy-start(f32[2,256]{1,0:T(2,128)} %gain.3) | copy-start | bytes 6148
  183.2 1.0 copy-start.4

commit v2 on v1

--- a/solution.py
+++ b/solution.py
@@ -294,6 +294,63 @@
     )(position, z_count, z_out, group_z, returned)
 
 
+def coordinates(axes, sizes, index):
+    ids = {}
+    for axis, size in reversed(list(zip(axes, sizes))):
+        ids[axis] = lax.rem(index, size)
+        index = index // size
+    return ids
+
+
+def direct_kernel(axes, sizes, split, reduce, x_ref, out_ref, *scratch):
+    *landing, send_sem, recv_sem = scratch
+    slots = landing[0] if reduce else out_ref
+    count = slots.shape[0]
+    me = jnp.int32(0)
+    for axis, size in zip(axes, sizes):
+        me = me * size + lax.axis_index(axis)
+    barrier = pltpu.get_barrier_semaphore()
+    peers = [coordinates(axes, sizes, lax.rem(me + k, count)) for k in range(1, count)]
+    for peer in peers:
+        pl.semaphore_signal(barrier, inc=1, device_id=peer, device_id_type=pl.DeviceIdType.MESH)
+    pl.semaphore_wait(barrier, count - 1)
+    copies = []
+    for k in range(1, count):
+        copy = pltpu.make_async_remote_copy(
+            src_ref=x_ref.at[lax.rem(me + k, count)] if split else x_ref,
+            dst_ref=slots.at[me],
+            send_sem=send_sem.at[k],
+            recv_sem=recv_sem.at[k],
+            device_id=peers[k - 1],
+            device_id_type=pl.DeviceIdType.MESH,
+        )
+        copy.start()
+        copies.append(copy)
+    slots[me] = x_ref[me] if split else x_ref[...]
+    for copy in copies:
+        copy.wait()
+    if reduce:
+        out_ref[...] = jnp.sum(slots[...], axis=0)
+
+
+def direct(x, axes, collective_id, split=False, reduce=False):
+    sizes = [lax.axis_size(axis) for axis in axes]
+    count = 1
+    for size in sizes:
+        count *= size
+    shape = x.shape if split or reduce else (count,) + x.shape
+    landing = [pltpu.VMEM((count,) + x.shape, x.dtype)] if reduce else []
+    return pl.pallas_call(
+        functools.partial(direct_kernel, axes, sizes, split, reduce),
+        in_specs=[VMEM],
+        out_specs=VMEM,
+        out_shape=jax.ShapeDtypeStruct(shape, x.dtype),
+        scratch_shapes=landing + [pltpu.SemaphoreType.DMA((count,)), pltpu.SemaphoreType.DMA((count,))],
+        compiler_params=params(collective_id=collective_id, has_side_effects=True),
+        name=f"direct_{collective_id}",
+    )(x)
+
+
 def shards(
     feats, z_count, hil_dest, pool_group,
     z_qkv, z_proj, z_up, z_down, z_gain,
@@ -310,7 +367,7 @@
 
     head = jnp.zeros((8, points), jnp.int32)
     head = head.at[0, :cells].set(hil_dest).at[1, 0].set(z_count[0])
-    everyone = lax.all_gather(jnp.concatenate([head, pool_group], axis=0), "gy", axis=0, tiled=False)
+    everyone = direct(jnp.concatenate([head, pool_group], axis=0), ("gy",), 0)
     all_dest = everyone[:, 0, :cells]
     all_count = everyone[:, 1, 0]
     group_all = everyone[:, 8:, :].reshape(row_devices * cells, points)
@@ -334,15 +391,17 @@
     ).reshape(cells, points, width)
 
     top, stats = pool(z_out, z_count, group_z, pool_w)
-    live = jnp.full((1, stats.shape[1]), z_count[0] * PGROUP, F32)
-    stats = lax.psum(jnp.concatenate([stats, live], axis=0), ("gx", "gy"))
+    live = jnp.full((6, stats.shape[1]), z_count[0] * PGROUP, F32)
+    stats = direct(jnp.concatenate([stats, live], axis=0), ("gx", "gy"), 1, reduce=True)
     average = stats[0] / stats[2]
     variance = stats[1] / stats[2] - average * average
     scales = jnp.stack([average, lax.rsqrt(variance + EPSILON), bn_gain])
     outgoing = batch_norm(top, position, scales, slots)
-    incoming = lax.all_to_all(outgoing, "gy", split_axis=0, concat_axis=0, tiled=True)
+    outgoing = outgoing.reshape((row_devices, capacity) + outgoing.shape[1:])
+    incoming = direct(outgoing, ("gy",), 2, split=True).reshape((slots,) + outgoing.shape[2:])
     lifted = p_block(incoming, anchor, live_h, p_gain, p_qkv, p_proj, p_up, p_down, unpool_w)
-    returned = lax.all_to_all(lifted, "gy", split_axis=0, concat_axis=0, tiled=True)
+    lifted = lifted.reshape((row_devices, capacity) + lifted.shape[1:])
+    returned = direct(lifted, ("gy",), 3, split=True).reshape((slots,) + lifted.shape[2:])
     return final(position, z_count, z_out, group_z, returned)
 
 

time: 239 us -> 182 us (0.76)
  blocking collectives: 89.7 us -> 0 us
  Pallas kernels: 112 us -> 173 us
  waiting for transfers between devices: 22.3 us -> 0 us
  starting transfers between devices: 6.05 us -> 0 us
    pallas_call x0 -> x4, Pallas kernels: none -> 61.8 us  [direct(): pl.pallas_call(functools.partial(direct_kernel, axes, sizes, split, reduc...]
    psum x1 -> x0, blocking collectives: 39.6 us -> none  [shards(): stats = lax.psum(jnp.concatenate([stats, live], axis=0), ('gx', 'gy'))]
    all_gather x1 -> x0, blocking collectives: 32.4 us -> none  [shards(): lax.all_gather(jnp.concatenate([head, pool_group], axis=0), 'gy', axis=0,...]
    all_to_all x1 -> x0, waiting for transfers between devices: 22.3 us -> none  [shards(): lax.all_to_all(outgoing, 'gy', split_axis=0, concat_axis=0, tiled=True)]
    all_to_all x1 -> x0, blocking collectives: 17.7 us -> none  [shards(): lax.all_to_all(lifted, 'gy', split_axis=0, concat_axis=0, tiled=True)]
    all_to_all x1 -> x0, starting transfers between devices: 6.05 us -> none  [shards(): lax.all_to_all(outgoing, 'gy', split_axis=0, concat_axis=0, tiled=True)]
  transfers between devices with their start and end apart: 1 -> 0, of which waited for: 1 -> 0; matrix products, arithmetic and copies ran while one was open for 1% -> 0% of each run, Pallas kernels for 0% -> 0%
where the time goes in v2:
time: 182 us; the launch traced here: 180 us
  Pallas kernels  173 us (95%)
  local copies, waits for them, and re-layouts  4.16 us (2%)
  other arithmetic  1.99 us (1%)
    pallas_call x1, Pallas kernels, z_block(): pl.pallas_call(functools.partial(z_kernel, cell_points), grid=(count // P...  67.1 us
    pallas_call x4, Pallas kernels, direct(): pl.pallas_call(functools.partial(direct_kernel, axes, sizes, split, reduc...  61.8 us
    pallas_call x1, Pallas kernels, p_block(): pl.pallas_call(p_kernel, grid=(rows // PATCH,), in_specs=[SMEM, SMEM] + [...  31.7 us
    pallas_call x1, Pallas kernels, pool(): pl.pallas_call(pool_kernel, in_specs=[SMEM, VMEM, VMEM, VMEM], out_specs=...  6.77 us
    pallas_call x1, Pallas kernels, final(): pl.pallas_call(final_kernel, in_specs=[SMEM, SMEM, VMEM, VMEM, VMEM], out...  4.74 us

profile of v2, /device:TPU:0, one launch (start us, length us, event | category | flops | bytes accessed | tf_op | source)
XLA Modules:
  0.0 180.2 jit_solution(2870141251636728454)
XLA Ops:
  0.7 0.0 copy-start.15
  0.7 0.0 copy-start.13
  0.7 0.6 copy-done.15
  1.3 0.2 convert_reduce_fusion.1
  1.6 0.1 scatter.9
  1.7 0.0 copy-done.13
  1.7 9.7 %direct_0.1 = s32[8,40,128]{2,1,0:T(8,128)S(1)} custom-call(s32[40,128]{1,0:T(8,128)S(1)} %pad_add_fusion.x_ref), custom_call_target="tpu_custom_call" | custom-call | tf_op jit(solution)/shard_map/direct_0/pallas_call | solution.py:343
  11.4 0.2 slice_reduce_fusion
  11.7 0.2 convert_reduce_fusion
  11.9 0.0 copy-start.6
  11.9 0.0 copy-start.10
  12.0 0.0 copy-start.5
  12.0 0.0 copy-start.8
  12.0 0.6 gather_fusion
  12.6 0.1 broadcast_select_fusion.group_ref
  12.6 0.1 add_select_fusion
  12.7 0.1 fusion.2
  12.8 1.2 select_reduce_fusion
  14.0 0.0 copy-start.12
  14.0 0.0 copy-done.6
  14.0 0.0 copy-done.10
  14.1 0.0 copy-done.5
  14.1 0.0 copy-done.8
  14.1 0.6 copy-done.12
  14.7 0.0 copy-start.1
  14.7 1.2 copy-done.1
  15.9 0.0 copy-start
  15.9 67.1 %z_block.1 = bf16[4096,128]{1,0:T(8,128)(2,1)S(1)} custom-call(s32[1]{0:T(128)} %copy.22.count_ref, bf16[4096,128]{1,0:T(8,128)(2,1)S(1)} %bitcast.22, f32[2,128]{1,0:T(2,128)S(1)} %copy-done.12, bf16[128,384]{1,0:T(8,128)(2,1)S(1)} %copy-done.8, bf16[128,128]{1,0:T(8,128)(2,1)S(1)} %copy-done.10, bf16[128,512]{1,0:T(8,128)(2,1)S(1)} %copy-done.5, ...), custom_call_target="tpu_custom_call" | custom-call | flops 35970351104 | bytes 2097152 | tf_op jit(solution)/shard_map/z_block/pallas_call | solution.py:152
  83.0 0.0 copy-done
  83.0 6.8 %pool.1 = (f32[32,32,256]{2,1,0:T(8,128)S(1)}, f32[2,256]{1,0:T(2,128)S(1)}) custom-call(s32[1]{0:T(128)} %copy.22.count_ref, bf16[32,128,128]{2,1,0:T(8,128)(2,1)S(1)} %bitcast.16, s32[32,128]{1,0:T(8,128)S(1)} %broadcast_select_fusion.group_ref, bf16[128,256]{1,0:T(8,128)(2,1)S(1)} %copy-done), custom_call_target="tpu_custom_call" | custom-call | tf_op jit(solution)/shard_map/pool/pallas_call | solution.py:197
  89.8 13.4 %direct_1.1 = f32[8,256]{1,0:T(8,128)S(1)} custom-call(f32[8,256]{1,0:T(8,128)S(1)} %concatenate.11.x_ref), custom_call_target="tpu_custom_call" | custom-call | tf_op jit(solution)/shard_map/direct_1/pallas_call | solution.py:343
  103.3 0.0 copy-start.14
  103.3 0.7 copy-done.14
  104.0 1.0 batch_norm.1
  104.9 0.0 copy-start.2
  105.0 0.0 copy-start.3
  105.0 0.0 copy-start.4
  105.0 0.0 copy-start.7
  105.0 0.0 copy-start.9
  105.0 0.0 copy-start.11
  105.0 20.5 %direct_2.1 = bf16[8,8,32,256]{3,2,1,0:T(8,128)(2,1)S(1)} custom-call(bf16[8,8,32,256]{3,2,1,0:T(8,128)(2,1)S(1)} %bitcast.18), custom_call_target="tpu_custom_call" | custom-call | tf_op jit(solution)/shard_map/direct_2/pallas_call | solution.py:343
  125.6 0.0 copy-done.2
  125.6 0.0 copy-done.3
  125.6 0.0 copy-done.4
  125.6 0.0 copy-done.7
  125.6 0.0 copy-done.9
  125.6 0.0 copy-done.11
  125.6 31.7 %p_block.1 = bf16[64,32,128]{2,1,0:T(8,128)(2,1)S(1)} custom-call(s32[32]{0:T(128)S(1)} %get-tuple-element.34.anchor_ref, s32[32]{0:T(128)S(1)} %get-tuple-element.33.live_ref, bf16[64,32,256]{2,1,0:T(8,128)(2,1)S(1)} %bitcast.20, f32[2,256]{1,0:T(2,128)S(1)} %copy-done.11, bf16[256,768]{1,0:T(8,128)(2,1)S(1)} %copy-done.4, bf16[256,256]{1,0:T(8,128)(2,1)S(1)} %copy-done.7, ...), custom_call_target="tpu_custom_call" | custom-call | flops 18790481920 | bytes 1048576 | tf_op jit(solution)/shard_map/p_block/pallas_call | solution.py:256
  157.3 18.1 %direct_3.1 = bf16[8,8,32,128]{3,2,1,0:T(8,128)(2,1)S(1)} custom-call(bf16[8,8,32,128]{3,2,1,0:T(8,128)(2,1)S(1)} %bitcast.21), custom_call_target="tpu_custom_call" | custom-call | tf_op jit(solution)/shard_map/direct_3/pallas_call | solution.py:343
  175.4 4.7 %final.1 = bf16[32,128,128]{2,1,0:T(8,128)(2,1)} custom-call(s32[32]{0:T(128)S(1)} %multiply_add_fusion.position_ref, s32[1]{0:T(128)} %copy.22.count_ref, bf16[32,128,128]{2,1,0:T(8,128)(2,1)S(1)} %bitcast.17, s32[32,128]{1,0:T(8,128)S(1)} %broadcast_select_fusion.group_ref, bf16[64,32,128]{2,1,0:T(8,128)(2,1)S(1)} %bitcast.19), custom_call_target="tpu_custom_call" | custom-call | tf_op jit(solution)/shard_map/final/pallas_call | solution.py:287
  (15 shorter events, 0.2 us)
Async XLA Ops:
  0.7 0.7 copy-start.15
  0.7 1.0 copy-start.13
  11.9 2.1 %copy-start.6 = (bf16[512,128]{1,0:T(8,128)(2,1)S(1)}, bf16[512,128]{1,0:T(8,128)(2,1)}, u32[]{:S(2)}) copy-start(bf16[512,128]{1,0:T(8,128)(2,1)} %down.2) | copy-start | bytes 393220
  11.9 2.1 %copy-start.10 = (bf16[128,128]{1,0:T(8,128)(2,1)S(1)}, bf16[128,128]{1,0:T(8,128)(2,1)}, u32[]{:S(2)}) copy-start(bf16[128,128]{1,0:T(8,128)(2,1)} %proj.2) | copy-start | bytes 98308
  12.0 2.1 %copy-start.5 = (bf16[128,512]{1,0:T(8,128)(2,1)S(1)}, bf16[128,512]{1,0:T(8,128)(2,1)}, u32[]{:S(2)}) copy-start(bf16[128,512]{1,0:T(8,128)(2,1)} %up.2) | copy-start | bytes 393220
  12.0 2.1 %copy-start.8 = (bf16[128,384]{1,0:T(8,128)(2,1)S(1)}, bf16[128,384]{1,0:T(8,128)(2,1)}, u32[]{:S(2)}) copy-start(bf16[128,384]{1,0:T(8,128)(2,1)} %qkv.2) | copy-start | bytes 294916
  14.0 0.7 copy-start.12
  14.7 1.2 copy-start.1
  15.9 67.1 %copy-start = (bf16[128,256]{1,0:T(8,128)(2,1)S(1)}, bf16[128,256]{1,0:T(8,128)(2,1)}, u32[]{:S(2)}) copy-start(bf16[128,256]{1,0:T(8,128)(2,1)} %pool_ref.1) | copy-start | bytes 196612
  103.3 0.7 copy-start.14
  104.9 20.6 %copy-start.2 = (bf16[256,1024]{1,0:T(8,128)(2,1)S(1)}, bf16[256,1024]{1,0:T(8,128)(2,1)}, u32[]{:S(2)}) copy-start(bf16[256,1024]{1,0:T(8,128)(2,1)} %up.3) | copy-start | bytes 1572868
  105.0 20.6 %copy-start.3 = (bf16[1024,256]{1,0:T(8,128)(2,1)S(1)}, bf16[1024,256]{1,0:T(8,128)(2,1)}, u32[]{:S(2)}) copy-start(bf16[1024,256]{1,0:T(8,128)(2,1)} %down.3) | copy-start | bytes 1572868
  105.0 20.6 %copy-start.4 = (bf16[256,768]{1,0:T(8,128)(2,1)S(1)}, bf16[256,768]{1,0:T(8,128)(2,1)}, u32[]{:S(2)}) copy-start(bf16[256,768]{1,0:T(8,128)(2,1)} %qkv.3) | copy-start | bytes 1179652
  105.0 20.6 %copy-start.7 = (bf16[256,256]{1,0:T(8,128)(2,1)S(1)}, bf16[256,256]{1,0:T(8,128)(2,1)}, u32[]{:S(2)}) copy-start(bf16[256,256]{1,0:T(8,128)(2,1)} %proj.3) | copy-start | bytes 393220
  105.0 20.6 %copy-start.9 = (bf16[256,128]{1,0:T(8,128)(2,1)S(1)}, bf16[256,128]{1,0:T(8,128)(2,1)}, u32[]{:S(2)}) copy-start(bf16[256,128]{1,0:T(8,128)(2,1)} %unpool.1) | copy-start | bytes 196612
  105.0 20.6 %copy-start.11 = (f32[2,256]{1,0:T(2,128)S(1)}, f32[2,256]{1,0:T(2,128)}, u32[]{:S(2)}) copy-start(f32[2,256]{1,0:T(2,128)} %gain.3) | copy-start | bytes 6148
